TPU v7x, 32 devices: a whole 2x2x4 slice. The times are simulated.
32 devices in a mesh: gx: 8 (over y, x, core), gy: 4 (over z).
Axes of the slice: x: 2, y: 2, z: 4, core: 2. Of those that a mesh axis runs over, the one named last changes fastest.
Arguments:
- fields: float32 [5, 128, 128, 128], P(None, 'gx', 'gy'), may hold values from -6 to 6
- patch_weight: bfloat16 [2560, 512], replicated, may hold values from -0.125 to 0.125
- trainer_of: int32 [2048, 1], P(('gx', 'gy')), may hold values from 0 to 31; in each aligned block of 64 rows (0 to 63, 64 to 127, ...) at most 4 rows name the same one
- lag_index: int32 [16, 16, 16], P('gx', 'gy'), may hold values from 0 to 1
- w_in: bfloat16 [32, 512, 2048], P(('gx', 'gy')), may hold values from -0.25 to 0.25
- b_in: float32 [32, 2048], P(('gx', 'gy')), may hold values from -3 to 3
- w_out: bfloat16 [32, 2048, 512], P(('gx', 'gy')), may hold values from -0.125 to 0.125
- b_out: float32 [32, 512], P(('gx', 'gy')), may hold values from -3 to 3
Outputs:
- new_fields: float32 [5, 128, 128, 128], P(None, 'gx', 'gy')
- patch_gradient: float32 [2560, 512], replicated
- w_in_gradient: float32 [32, 512, 2048], P(('gx', 'gy'))
- b_in_gradient: float32 [32, 2048], P(('gx', 'gy'))
- w_out_gradient: float32 [32, 2048, 512], P(('gx', 'gy'))
- b_out_gradient: float32 [32, 512], P(('gx', 'gy'))
Inputs may be any that keep to these rules, and one draw needn't show every extreme that they name: `trainer_of`: among the 64 rows of one brick, no trainer is named more than 4 times.
All inputs are finite; a program needn't handle non-finite values.
Results may differ from a plain program's by a relative error of at most 0.0062.
Values may be sent and summed in bfloat16 or wider, within the bound.
A program may use at most 128 MiB of HBM per device.

v0:
```python
import jax
import jax.numpy as jnp
from jax import lax
from jax.sharding import PartitionSpec as P

FIELDS = 5
PATCH = 8
STEPS = 3
EMBED = 512
BLOCK_ROWS = 2
time_step = 0.2
viscosity = 0.5
drift_x = 0.6
drift_y = -0.4
drift_z = 0.3
error_weight = 0.0625


def with_halo(cells, sides, width):
    for axis, dim in sides:
        count = lax.axis_size(axis)
        ends = count - 1
        head = lax.slice_in_dim(cells, 0, width, axis=dim)
        tail = lax.slice_in_dim(cells, cells.shape[dim] - width, cells.shape[dim], axis=dim)
        cells = jnp.concatenate(
            [
                lax.ppermute(tail, axis, [(i, (i + 1) % count) for i in range(ends)]),
                cells,
                lax.ppermute(head, axis, [((i + 1) % count, i) for i in range(ends)]),
            ],
            axis=dim,
        )
    return cells


def shifted(padded, dimension, offset):
    window = [slice(None)]
    for other in (1, 2, 3):
        window.append(slice(2, padded.shape[other] - 2))
    window[dimension] = slice(2 + offset, padded.shape[dimension] - 2 + offset)
    return padded[tuple(window)]


def tendency(padded):
    gradients = []
    laplacian = 0.0
    for dimension in (1, 2, 3):
        back_two = shifted(padded, dimension, -2)
        back_one = shifted(padded, dimension, -1)
        middle = shifted(padded, dimension, 0)
        ahead_one = shifted(padded, dimension, 1)
        ahead_two = shifted(padded, dimension, 2)
        gradients.append((back_two - 8.0 * back_one + 8.0 * ahead_one - ahead_two) / 12.0)
        laplacian = (
            laplacian
            + (-back_two + 16.0 * back_one - 30.0 * middle + 16.0 * ahead_one - ahead_two) / 12.0
        )
    carried = drift_x * gradients[0] + drift_y * gradients[1] + drift_z * gradients[2]
    divergence = gradients[0][1] + gradients[1][2] + gradients[2][3]
    acoustic = jnp.stack(
        [divergence, gradients[0][4], gradients[1][4], gradients[2][4], divergence]
    )
    return viscosity * laplacian - carried - acoustic


def contract_rows(left, right):
    return lax.dot_general(
        left, right, (((0,), (0,)), ((), ())), preferred_element_type=jnp.float32
    )


def contract_cols(left, right):
    return lax.dot_general(
        left, right, (((1,), (1,)), ((), ())), preferred_element_type=jnp.float32
    )


def trainer_step(source, target, valid, w_first, b_first, w_second, b_second):
    pre = jnp.dot(source, w_first, preferred_element_type=jnp.float32) + b_first
    hidden = jax.nn.silu(pre).astype(jnp.bfloat16)
    predict = jnp.dot(hidden, w_second, preferred_element_type=jnp.float32) + b_second
    error = (error_weight * (predict - target.astype(jnp.float32)) * valid).astype(jnp.bfloat16)
    b_second_grad = jnp.sum(error.astype(jnp.float32), axis=0)
    w_second_grad = contract_rows(hidden, error)
    back = contract_cols(error, w_second)
    sigma = jax.nn.sigmoid(pre)
    pre_grad = (back * sigma * (1.0 + pre * (1.0 - sigma))).astype(jnp.bfloat16)
    b_first_grad = jnp.sum(pre_grad.astype(jnp.float32), axis=0)
    w_first_grad = contract_rows(source, pre_grad)
    source_grad = contract_cols(pre_grad, w_first).astype(jnp.bfloat16)
    return (source_grad, w_first_grad, b_first_grad, w_second_grad, b_second_grad)


def patchify(state):
    width_x, width_y, width_z = (state.shape[1], state.shape[2], state.shape[3])
    shaped = state.reshape(
        FIELDS, width_x // PATCH, PATCH, width_y // PATCH, PATCH, width_z // PATCH, PATCH
    )
    return shaped.transpose(1, 3, 5, 0, 2, 4, 6).reshape(-1, FIELDS * PATCH**3)


def pad_third(current):
    return jnp.pad(current, ((0, 0), (0, 0), (0, 0), (2, 2)))


def advance(fields):
    states = []
    current = fields
    for counter in range(STEPS):
        padded = with_halo(current, (("gx", 1), ("gy", 2)), 2)
        current = current + time_step * tendency(pad_third(padded))
        states.append(current)
    return states


def per_device(fields, patch_weight, trainer_of, lag_index, w_in, b_in, w_out, b_out):
    states = advance(fields)
    devices = lax.axis_size("gx") * lax.axis_size("gy")
    lag_rows = lag_index.reshape(-1, 1)
    picked = patchify(states[0].astype(jnp.bfloat16))
    picked = jnp.where(lag_rows == 1, patchify(states[1].astype(jnp.bfloat16)), picked)
    target = jnp.dot(
        patchify(states[-1].astype(jnp.bfloat16)), patch_weight, preferred_element_type=jnp.float32
    ).astype(jnp.bfloat16)
    patch_count = picked.shape[0]
    block_count = patch_count // BLOCK_ROWS
    slot_count = max(2, 2 * block_count // devices)
    owners = trainer_of[:, 0]
    onehot = (owners[:, None] == jnp.arange(devices, dtype=jnp.int32)[None, :]).astype(jnp.int32)
    within_rank = jnp.sum((jnp.cumsum(onehot, axis=0) - onehot) * onehot, axis=1)
    block_slot = owners * slot_count + within_rank

    def into_slots(rows):
        width = rows.shape[1]
        blocks = rows.reshape(block_count, BLOCK_ROWS, width)
        buffer = (
            jnp.zeros((devices * slot_count, BLOCK_ROWS, width), rows.dtype)
            .at[block_slot]
            .set(blocks)
        )
        return buffer.reshape(devices, slot_count, BLOCK_ROWS, width)

    valid_send = jnp.zeros((devices * slot_count,), jnp.bfloat16).at[block_slot].set(1.0)
    valid_send = valid_send.reshape(devices, slot_count)
    got_patches, got_target, got_valid = (
        lax.all_to_all(into_slots(picked), ("gx", "gy"), split_axis=0, concat_axis=0, tiled=True),
        lax.all_to_all(into_slots(target), ("gx", "gy"), split_axis=0, concat_axis=0, tiled=True),
        lax.all_to_all(valid_send, ("gx", "gy"), split_axis=0, concat_axis=0, tiled=True),
    )
    flat_patches = got_patches.reshape(-1, FIELDS * PATCH**3)
    source = jnp.dot(flat_patches, patch_weight, preferred_element_type=jnp.float32).astype(
        jnp.bfloat16
    )
    valid_rows = jnp.repeat(got_valid.astype(jnp.float32).reshape(-1), BLOCK_ROWS)[:, None]
    results = trainer_step(
        source, got_target.reshape(-1, EMBED), valid_rows, w_in[0], b_in[0], w_out[0], b_out[0]
    )
    partial_value = contract_rows(flat_patches, results[0])
    patch_gradient = lax.psum(partial_value, ("gx", "gy"))
    return (
        states[-1],
        patch_gradient,
        results[1][None],
        results[2][None],
        results[3][None],
        results[4][None],
    )


def solution(mesh):
    in_specs = (
        P(None, "gx", "gy", None),
        P(),
        P(("gx", "gy"), None),
        P("gx", "gy", None),
        P(("gx", "gy"), None, None),
        P(("gx", "gy"), None),
        P(("gx", "gy"), None, None),
        P(("gx", "gy"), None),
    )
    out_specs = (
        P(None, "gx", "gy", None),
        P(),
        P(("gx", "gy"), None, None),
        P(("gx", "gy"), None),
        P(("gx", "gy"), None, None),
        P(("gx", "gy"), None),
    )
    return jax.shard_map(
        per_device, mesh=mesh, in_specs=in_specs, out_specs=out_specs, check_vma=False
    )
```

profile of v0, /device:TPU:0, one launch (start us, length us, event | category | flops | bytes accessed | tf_op | source)
XLA Modules:
  0.0 457.9 jit_solution(11400775036131845433)
XLA Ops:
  16.3 3.8 collective-permute-start.2
  22.3 4.3 collective-permute-done.3
  31.9 4.0 fusion.57
  37.0 4.0 collective-permute-start.4
  44.1 8.5 %all-to-all-start.2 = ((bf16[32,1,4]{2,1,0:T(2,128)(2,1)}), bf16[32,1,4]{2,1,0:T(2,128)(2,1)S(1)}, u32[]{:S(2)}, u32[]{:S(2)}) async-start(bf16[32,1,4]{2,1,0:T(2,128)(2,1)} %all_to_all.16), calls=%async_computation.2 | async-start | bytes 32768 | tf_op jit(solution)/shard_map/all_to_all | solution.py:148
  53.9 3.7 collective-permute-start.6
  59.9 4.2 collective-permute-done.7
  64.1 3.5 select_maximum_fusion.4
  69.8 3.9 fusion.59
  78.6 14.4 %reshape.78 = bf16[5,2,8,4,8,16,8]{6,5,4,3,2,1,0:T(8,128)(2,1)} reshape(bf16[5,16,32,128]{3,2,1,0:T(8,128)(2,1)} %get-tuple-element.8) | data formatting | bytes 1310720 | tf_op jit(solution)/shard_map/reshape | solution.py:96
  93.1 10.7 %copy.18 = bf16[2,4,16,5,8,8,8]{6,5,4,3,2,1,0:T(8,128)(2,1)} copy(bf16[2,4,16,5,8,8,8]{6,2,5,1,4,0,3:T(8,128)(2,1)} %bitcast.69) | data formatting | bytes 1310720 | tf_op jit(solution)/shard_map/transpose | solution.py:99
  103.8 14.5 %reshape.79 = bf16[64,2,2560]{2,1,0:T(2,128)(2,1)} reshape(bf16[2,4,16,5,8,8,8]{6,5,4,3,2,1,0:T(8,128)(2,1)} %copy.18) | data formatting | bytes 1310720 | tf_op jit(solution)/shard_map/reshape | solution.py:99
  118.3 14.4 %reshape.76 = bf16[5,2,8,4,8,16,8]{6,5,4,3,2,1,0:T(8,128)(2,1)} reshape(bf16[5,16,32,128]{3,2,1,0:T(8,128)(2,1)} %get-tuple-element.10) | data formatting | bytes 1310720 | tf_op jit(solution)/shard_map/reshape | solution.py:96
  132.7 10.6 %copy.17 = bf16[2,4,16,5,8,8,8]{6,5,4,3,2,1,0:T(8,128)(2,1)} copy(bf16[2,4,16,5,8,8,8]{6,2,5,1,4,0,3:T(8,128)(2,1)} %bitcast.70) | data formatting | bytes 1310720 | tf_op jit(solution)/shard_map/transpose | solution.py:99
  143.3 14.5 %reshape.77 = bf16[64,2,2560]{2,1,0:T(2,128)(2,1)} reshape(bf16[2,4,16,5,8,8,8]{6,5,4,3,2,1,0:T(8,128)(2,1)} %copy.17) | data formatting | bytes 1310720 | tf_op jit(solution)/shard_map/reshape | solution.py:99
  159.1 3.4 collective-permute-start.10
  164.7 4.3 collective-permute-done.11
  169.0 3.5 select_maximum_fusion
  174.8 4.1 fusion.55
  178.9 14.4 %reshape.82 = bf16[5,2,8,4,8,16,8]{6,5,4,3,2,1,0:T(8,128)(2,1)} reshape(bf16[5,16,32,128]{3,2,1,0:T(8,128)(2,1)} %get-tuple-element.6) | data formatting | bytes 1310720 | tf_op jit(solution)/shard_map/reshape | solution.py:96
  193.3 13.3 %copy.19 = bf16[2,4,16,5,8,8,8]{2,1,0,6,5,4,3:T(4,128)(2,1)} copy(bf16[2,4,16,5,8,8,8]{6,2,5,1,4,0,3:T(8,128)(2,1)} %bitcast.71) | data formatting | bytes 1310720 | tf_op jit(solution)/shard_map/transpose | solution.py:99
  206.6 7.3 %reshape.83 = bf16[128,2560]{0,1:T(8,128)(2,1)S(1)} reshape(bf16[2,4,16,5,8,8,8]{2,1,0,6,5,4,3:T(4,128)(2,1)} %copy.19) | data formatting | bytes 1310720 | tf_op jit(solution)/shard_map/reshape | solution.py:99
  215.4 7.8 %scatter_fusion.1 = bf16[128,2,512]{2,1,0:T(2,128)(2,1)} fusion(bf16[128,2,512]{2,1,0:T(2,128)(2,1)} %broadcast_in_dim.41, s32[64]{0:T(128)S(1)} %fusion.52, bf16[64,2,512]{2,1,0:T(2,128)(2,1)S(1)} %reshape.99), kind=kCustom, calls=%fused_computation.1 | custom fusion | bytes 393472 | tf_op jit(solution)/shard_map/scatter | solution.py:139
  223.3 6.9 %all-to-all-start.1 = ((bf16[32,4,2,512]{3,2,1,0:T(2,128)(2,1)}), bf16[32,4,2,512]{3,2,1,0:T(2,128)(2,1)S(1)}, u32[]{:S(2)}, u32[]{:S(2)}) async-start(bf16[32,4,2,512]{3,2,1,0:T(2,128)(2,1)} %bitcast.11), calls=%async_computation.1 | async-start | bytes 524288 | tf_op jit(solution)/shard_map/all_to_all | solution.py:147
  234.0 8.2 %scatter_fusion = bf16[128,2,2560]{2,1,0:T(2,128)(2,1)} fusion(bf16[128,2,2560]{2,1,0:T(2,128)(2,1)} %broadcast_in_dim.39, s32[64]{0:T(128)} %copy-done.13, bf16[64,2,2560]{2,1,0:T(2,128)(2,1)S(1)} %broadcast_select_fusion), kind=kCustom, calls=%fused_computation | custom fusion | bytes 1966336 | tf_op jit(solution)/shard_map/scatter | solution.py:139
  242.2 6.1 %all-to-all-start = ((bf16[32,4,2,2560]{3,2,1,0:T(2,128)(2,1)}), bf16[32,4,2,2560]{3,2,1,0:T(2,128)(2,1)}, u32[]{:S(2)}, u32[]{:S(2)}) async-start(bf16[32,4,2,2560]{3,2,1,0:T(2,128)(2,1)} %bitcast.72), calls=%async_computation | async-start | bytes 2621440 | tf_op jit(solution)/shard_map/all_to_all | solution.py:146
  249.6 29.0 %all-to-all-done = bf16[32,4,2,2560]{3,2,1,0:T(2,128)(2,1)} async-done(((bf16[32,4,2,2560]{3,2,1,0:T(2,128)(2,1)}), bf16[32,4,2,2560]{3,2,1,0:T(2,128)(2,1)}, u32[]{:S(2)}, u32[]{:S(2)}) %all-to-all-start) | async-done | bytes 1310752 | tf_op jit(solution)/shard_map/all_to_all | solution.py:146
  278.7 4.1 reshape.81
  291.0 6.2 %fusion.46 = f32[2560,512]{1,0:T(8,128)} fusion(bf16[256,2560]{1,0:T(8,128)(2,1)} %reshape.81, bf16[256,2048]{1,0:T(8,128)(2,1)} %get-tuple-element.48, bf16[1,512,2048]{2,1,0:T(8,128)(2,1)} %param.12), kind=kOutput, calls=%fused_computation.96 | convolution fusion | flops 1208090624 | bytes 9699328 | tf_op jit(solution)/shard_map/dot_general | solution.py:67
  297.2 4.1 convolution_bitcast_fusion.1
  304.2 141.2 %all-reduce.5.cloned.1.call-done = f32[2560,512]{1,0:T(8,128)} async-done(((f32[2560,512]{1,0:T(8,128)}), f32[2560,512]{1,0:T(8,128)}) %all-reduce.5.cloned.1.call-update) | async-done | bytes 5242896 | tf_op jit(solution)/shard_map/psum | solution.py:159
  445.4 5.4 %copy.40 = f32[2560,512]{1,0:T(8,128)} copy(f32[2560,512]{1,0:T(8,128)} %all-reduce.5.cloned.1.call-done) | data formatting | bytes 10485760
  (112 shorter events, 54.5 us)
Async XLA Ops:
  7.2 206.8 %copy-start = (bf16[2560,512]{1,0:T(8,128)(2,1)S(1)}, bf16[2560,512]{1,0:T(8,128)(2,1)}, u32[]{:S(2)}) copy-start(bf16[2560,512]{1,0:T(8,128)(2,1)} %param.9) | copy-start | bytes 7864324
  8.4 5.4 %collective-permute-start = (f32[5,2,32,128]{3,2,1,0:T(8,128)S(1)}, f32[5,2,32,128]{3,2,1,0:T(8,128)S(1)}, u32[]{:S(2)}, u32[]{:S(2)}) collective-permute-start(f32[5,2,32,128]{3,2,1,0:T(8,128)S(1)} %get-tuple-element.42), channel_id=1, source_target_pairs={{0,4},{4,8},{8,12},{12,16},{16,20},{20,24},{24,28},{1,5},{5,9},{9,... | collective-permute-start | bytes 491528 | tf_op jit(solution)/shard_map/ppermute | solution.py:27
  10.8 5.4 %collective-permute-start.1 = (f32[5,2,32,128]{3,2,1,0:T(8,128)S(1)}, f32[5,2,32,128]{3,2,1,0:T(8,128)S(1)}, u32[]{:S(2)}, u32[]{:S(2)}) collective-permute-start(f32[5,2,32,128]{3,2,1,0:T(8,128)S(1)} %get-tuple-element.41), channel_id=1, source_target_pairs={{4,0},{8,4},{12,8},{16,12},{20,16},{24,20},{28,24},{5,1},{9,5},{13... | collective-permute-start | bytes 491528 | tf_op jit(solution)/shard_map/ppermute | solution.py:29
  16.3 6.0 %collective-permute-start.2 = (f32[5,20,2,128]{3,2,1,0:T(2,128)S(1)}, f32[5,20,2,128]{3,2,1,0:T(2,128)S(1)}, u32[]{:S(2)}, u32[]{:S(2)}) collective-permute-start(f32[5,20,2,128]{3,2,1,0:T(2,128)S(1)} %get-tuple-element.32), channel_id=1, source_target_pairs={{0,1},{1,2},{2,3},{4,5},{5,6},{6,7},{8,9},{9,10},{10,11},{12,13},{... | collective-permute-start | bytes 307208 | tf_op jit(solution)/shard_map/ppermute | solution.py:27
  20.1 6.6 %collective-permute-start.3 = (f32[5,20,2,128]{3,2,1,0:T(2,128)S(1)}, f32[5,20,2,128]{3,2,1,0:T(2,128)S(1)}, u32[]{:S(2)}, u32[]{:S(2)}) collective-permute-start(f32[5,20,2,128]{3,2,1,0:T(2,128)S(1)} %get-tuple-element.33), channel_id=1, source_target_pairs={{1,0},{2,1},{3,2},{5,4},{6,5},{7,6},{9,8},{10,9},{11,10},{13,12},{... | collective-permute-start | bytes 307208 | tf_op jit(solution)/shard_map/ppermute | solution.py:29
  30.6 1.3 copy-start.6
  31.9 10.4 %copy-start.12 = (s32[64,1]{0,1:T(1,128)S(1)}, s32[64,1]{0,1:T(1,128)}, u32[]{:S(2)}) copy-start(s32[64,1]{0,1:T(1,128)} %param.10) | copy-start | bytes 772
  35.9 1.1 copy-start.3
  37.0 15.6 %collective-permute-start.4 = (f32[5,2,32,128]{3,2,1,0:T(8,128)S(1)}, f32[5,2,32,128]{3,2,1,0:T(8,128)S(1)}, u32[]{:S(2)}, u32[]{:S(2)}) collective-permute-start(f32[5,2,32,128]{3,2,1,0:T(8,128)S(1)} %get-tuple-element.36), channel_id=1, source_target_pairs={{0,4},{4,8},{8,12},{12,16},{16,20},{20,24},{24,28},{1,5},{5,9},{9,... | collective-permute-start | bytes 491528 | tf_op jit(solution)/shard_map/ppermute | solution.py:27
  41.0 11.5 %collective-permute-start.5 = (f32[5,2,32,128]{3,2,1,0:T(8,128)S(1)}, f32[5,2,32,128]{3,2,1,0:T(8,128)S(1)}, u32[]{:S(2)}, u32[]{:S(2)}) collective-permute-start(f32[5,2,32,128]{3,2,1,0:T(8,128)S(1)} %get-tuple-element.37), channel_id=1, source_target_pairs={{4,0},{8,4},{12,8},{16,12},{20,16},{24,20},{28,24},{5,1},{9,5},{13... | collective-permute-start | bytes 491528 | tf_op jit(solution)/shard_map/ppermute | solution.py:29
  42.4 173.1 %copy-start.13 = (s32[64]{0:T(128)}, s32[64]{0:T(128)S(1)}, u32[]{:S(2)}) copy-start(s32[64]{0:T(128)S(1)} %fusion.52) | copy-start | bytes 772
  44.1 179.2 %all-to-all-start.2 = ((bf16[32,1,4]{2,1,0:T(2,128)(2,1)}), bf16[32,1,4]{2,1,0:T(2,128)(2,1)S(1)}, u32[]{:S(2)}, u32[]{:S(2)}) async-start(bf16[32,1,4]{2,1,0:T(2,128)(2,1)} %all_to_all.16), calls=%async_computation.2 | async-start | bytes 32768 | tf_op jit(solution)/shard_map/all_to_all | solution.py:148
  52.6 6.6 %copy-start.4 = (f32[5,16,32,128]{3,2,1,0:T(8,128)S(1)}, f32[5,16,32,128]{3,2,1,0:T(8,128)}, u32[]{:S(2)}) copy-start(f32[5,16,32,128]{3,2,1,0:T(8,128)} %copy-done.3) | copy-start | bytes 3932164
  53.9 6.1 %collective-permute-start.6 = (f32[5,20,2,128]{3,2,1,0:T(2,128)S(1)}, f32[5,20,2,128]{3,2,1,0:T(2,128)S(1)}, u32[]{:S(2)}, u32[]{:S(2)}) collective-permute-start(f32[5,20,2,128]{3,2,1,0:T(2,128)S(1)} %get-tuple-element.30), channel_id=1, source_target_pairs={{0,1},{1,2},{2,3},{4,5},{5,6},{6,7},{8,9},{9,10},{10,11},{12,13},{... | collective-permute-start | bytes 307208 | tf_op jit(solution)/shard_map/ppermute | solution.py:27
  57.5 6.6 %collective-permute-start.7 = (f32[5,20,2,128]{3,2,1,0:T(2,128)S(1)}, f32[5,20,2,128]{3,2,1,0:T(2,128)S(1)}, u32[]{:S(2)}, u32[]{:S(2)}) collective-permute-start(f32[5,20,2,128]{3,2,1,0:T(2,128)S(1)} %get-tuple-element.31), channel_id=1, source_target_pairs={{1,0},{2,1},{3,2},{5,4},{6,5},{7,6},{9,8},{10,9},{11,10},{13,12},{... | collective-permute-start | bytes 307208 | tf_op jit(solution)/shard_map/ppermute | solution.py:29
  69.8 8.1 %copy-start.11 = (s32[2,4,16]{2,1,0:T(4,128)S(1)}, s32[2,4,16]{2,1,0:T(4,128)}, u32[]{:S(2)}) copy-start(s32[2,4,16]{2,1,0:T(4,128)} %param.11) | copy-start | bytes 1540
  73.7 1.1 copy-start.1
  74.8 83.0 %collective-permute-start.8 = (f32[5,2,32,128]{3,2,1,0:T(8,128)S(1)}, f32[5,2,32,128]{3,2,1,0:T(8,128)S(1)}, u32[]{:S(2)}, u32[]{:S(2)}) collective-permute-start(f32[5,2,32,128]{3,2,1,0:T(8,128)S(1)} %get-tuple-element.34), channel_id=1, source_target_pairs={{0,4},{4,8},{8,12},{12,16},{16,20},{20,24},{24,28},{1,5},{5,9},{9,... | collective-permute-start | bytes 491528 | tf_op jit(solution)/shard_map/ppermute | solution.py:27
  76.1 81.7 %collective-permute-start.9 = (f32[5,2,32,128]{3,2,1,0:T(8,128)S(1)}, f32[5,2,32,128]{3,2,1,0:T(8,128)S(1)}, u32[]{:S(2)}, u32[]{:S(2)}) collective-permute-start(f32[5,2,32,128]{3,2,1,0:T(8,128)S(1)} %get-tuple-element.35), channel_id=1, source_target_pairs={{4,0},{8,4},{12,8},{16,12},{20,16},{24,20},{28,24},{5,1},{9,5},{13... | collective-permute-start | bytes 491528 | tf_op jit(solution)/shard_map/ppermute | solution.py:29
  157.8 6.1 %copy-start.2 = (f32[5,16,32,128]{3,2,1,0:T(8,128)S(1)}, f32[5,16,32,128]{3,2,1,0:T(8,128)}, u32[]{:S(2)}) copy-start(f32[5,16,32,128]{3,2,1,0:T(8,128)} %copy-done.1) | copy-start | bytes 3932164
  159.1 5.6 %collective-permute-start.10 = (f32[5,20,2,128]{3,2,1,0:T(2,128)S(1)}, f32[5,20,2,128]{3,2,1,0:T(2,128)S(1)}, u32[]{:S(2)}, u32[]{:S(2)}) collective-permute-start(f32[5,20,2,128]{3,2,1,0:T(2,128)S(1)} %get-tuple-element.26), channel_id=1, source_target_pairs={{0,1},{1,2},{2,3},{4,5},{5,6},{6,7},{8,9},{9,10},{10,11},{12,13},{... | collective-permute-start | bytes 307208 | tf_op jit(solution)/shard_map/ppermute | solution.py:27
  162.5 6.6 %collective-permute-start.11 = (f32[5,20,2,128]{3,2,1,0:T(2,128)S(1)}, f32[5,20,2,128]{3,2,1,0:T(2,128)S(1)}, u32[]{:S(2)}, u32[]{:S(2)}) collective-permute-start(f32[5,20,2,128]{3,2,1,0:T(2,128)S(1)} %get-tuple-element.27), channel_id=1, source_target_pairs={{1,0},{2,1},{3,2},{5,4},{6,5},{7,6},{9,8},{10,9},{11,10},{13,12},{... | collective-permute-start | bytes 307208 | tf_op jit(solution)/shard_map/ppermute | solution.py:29
  223.3 19.0 %all-to-all-start.1 = ((bf16[32,4,2,512]{3,2,1,0:T(2,128)(2,1)}), bf16[32,4,2,512]{3,2,1,0:T(2,128)(2,1)S(1)}, u32[]{:S(2)}, u32[]{:S(2)}) async-start(bf16[32,4,2,512]{3,2,1,0:T(2,128)(2,1)} %bitcast.11), calls=%async_computation.1 | async-start | bytes 524288 | tf_op jit(solution)/shard_map/all_to_all | solution.py:147
  242.2 36.4 %all-to-all-start = ((bf16[32,4,2,2560]{3,2,1,0:T(2,128)(2,1)}), bf16[32,4,2,2560]{3,2,1,0:T(2,128)(2,1)}, u32[]{:S(2)}, u32[]{:S(2)}) async-start(bf16[32,4,2,2560]{3,2,1,0:T(2,128)(2,1)} %bitcast.72), calls=%async_computation | async-start | bytes 2621440 | tf_op jit(solution)/shard_map/all_to_all | solution.py:146
  248.3 197.1 %all-reduce.5.cloned.1.call-start = ((), (), s32[]{:S(2)}) async-start(), calls=%async_computation.3 | async-start | bytes 10485760 | tf_op jit(solution)/shard_map/psum | solution.py:159
  282.7 2.3 copy-start.5
  282.7 2.3 copy-start.10
  285.1 1.0 copy-start.9
  285.1 1.8 copy-start.14
  285.1 1.8 copy-start.15
  285.8 2.4 copy-start.7
  297.2 4.1 copy-start.8
Sparse Core Ops, SparseCore 0:
  297.3 148.0 all-reduce.4
where the time goes:
time: 466 us; the launch traced here: 458 us
  waiting for transfers between devices  185 us (40%)
  local copies, waits for them, and re-layouts  154 us (33%)
  starting transfers between devices  48.8 us (10%)
  other arithmetic  34.4 us (7%)
  matrix products  20.8 us (4%)
  between operations  14.9 us (3%)
    psum x1, waiting for transfers between devices, per_device(): patch_gradient = lax.psum(partial_value, ('gx', 'gy'))  141 us
    reshape x3, local copies, waits for them, and re-layouts, patchify(): state.reshape(FIELDS, width_x // PATCH, PATCH, width_y // PATCH, PATCH, w...  43.3 us
    reshape x3, local copies, waits for them, and re-layouts, patchify(): shaped.transpose(1, 3, 5, 0, 2, 4, 6).reshape(-1, FIELDS * PATCH ** 3)  36.3 us
    transpose x3, local copies, waits for them, and re-layouts, patchify(): shaped.transpose(1, 3, 5, 0, 2, 4, 6).reshape(-1, FIELDS * PATCH ** 3)  34.6 us
    all_to_all x1, waiting for transfers between devices, per_device(): lax.all_to_all(into_slots(picked), ('gx', 'gy'), split_axis=0, concat_axi...  29 us
    ppermute x6, starting transfers between devices, with_halo(): lax.ppermute(tail, axis, [(i, (i + 1) % count) for i in range(ends)])  18.6 us
    scatter x2, local copies, waits for them, and re-layouts, into_slots(): buffer = jnp.zeros((devices * slot_count, BLOCK_ROWS, width), rows.dtype)...  16 us
    ppermute x6, waiting for transfers between devices, with_halo(): lax.ppermute(head, axis, [((i + 1) % count, i) for i in range(ends)])  13.3 us
  transfers between devices with their start and end apart: 16, of which 9 were waited for; matrix products, arithmetic and copies ran while one was open for 37% of the time, Pallas kernels for 0%

commit v1 on v0

--- a/solution.py
+++ b/solution.py
@@ -156,7 +156,7 @@
         source, got_target.reshape(-1, EMBED), valid_rows, w_in[0], b_in[0], w_out[0], b_out[0]
     )
     partial_value = contract_rows(flat_patches, results[0])
-    patch_gradient = lax.psum(partial_value, ("gx", "gy"))
+    patch_gradient = jax.lax.psum(jax.lax.psum(partial_value, "gx"), "gy")
     return (
         states[-1],
         patch_gradient,

time: 466 us -> 601 us (1.29)
  waiting for transfers between devices: 185 us -> 321 us
    psum x1 -> x2, waiting for transfers between devices: 141 us -> 277 us  [per_device(): patch_gradient = jax.lax.psum(jax.lax.psum(partial_value, 'gx'), 'gy')]
  transfers between devices with their start and end apart: 16 -> 17, of which waited for: 9 -> 10; matrix products, arithmetic and copies ran while one was open for 37% -> 29% of each run, Pallas kernels for 0% -> 0%
where the time goes in v1:
time: 601 us; the launch traced here: 594 us
  waiting for transfers between devices  321 us (53%)
  local copies, waits for them, and re-layouts  154 us (26%)
  starting transfers between devices  48.8 us (8%)
  other arithmetic  34.4 us (6%)
  matrix products  20.8 us (3%)
  between operations  14.9 us (2%)
    psum x2, waiting for transfers between devices, per_device(): patch_gradient = jax.lax.psum(jax.lax.psum(partial_value, 'gx'), 'gy')  277 us
    reshape x3, local copies, waits for them, and re-layouts, patchify(): state.reshape(FIELDS, width_x // PATCH, PATCH, width_y // PATCH, PATCH, w...  43.3 us
    reshape x3, local copies, waits for them, and re-layouts, patchify(): shaped.transpose(1, 3, 5, 0, 2, 4, 6).reshape(-1, FIELDS * PATCH ** 3)  36.3 us
    transpose x3, local copies, waits for them, and re-layouts, patchify(): shaped.transpose(1, 3, 5, 0, 2, 4, 6).reshape(-1, FIELDS * PATCH ** 3)  34.6 us
    all_to_all x1, waiting for transfers between devices, per_device(): lax.all_to_all(into_slots(picked), ('gx', 'gy'), split_axis=0, concat_axi...  29 us
    ppermute x6, starting transfers between devices, with_halo(): lax.ppermute(tail, axis, [(i, (i + 1) % count) for i in range(ends)])  18.6 us
    scatter x2, local copies, waits for them, and re-layouts, into_slots(): buffer = jnp.zeros((devices * slot_count, BLOCK_ROWS, width), rows.dtype)...  16 us
    ppermute x6, waiting for transfers between devices, with_halo(): lax.ppermute(head, axis, [((i + 1) % count, i) for i in range(ends)])  13.3 us
  transfers between devices with their start and end apart: 17, of which 10 were waited for; matrix products, arithmetic and copies ran while one was open for 29% of the time, Pallas kernels for 0%

profile of v1, /device:TPU:0, one launch (start us, length us, event | category | flops | bytes accessed | tf_op | source)
XLA Modules:
  0.0 593.6 jit_solution(2547997327838988676)
XLA Ops:
  16.3 3.8 collective-permute-start.2
  22.3 4.3 collective-permute-done.3
  31.9 4.0 fusion.57
  37.0 4.0 collective-permute-start.4
  44.1 8.5 %all-to-all-start.2 = ((bf16[32,1,4]{2,1,0:T(2,128)(2,1)}), bf16[32,1,4]{2,1,0:T(2,128)(2,1)S(1)}, u32[]{:S(2)}, u32[]{:S(2)}) async-start(bf16[32,1,4]{2,1,0:T(2,128)(2,1)} %all_to_all.16), calls=%async_computation.2 | async-start | bytes 32768 | tf_op jit(solution)/shard_map/all_to_all | solution.py:148
  53.9 3.7 collective-permute-start.6
  59.9 4.2 collective-permute-done.7
  64.1 3.5 select_maximum_fusion.4
  69.8 3.9 fusion.59
  78.6 14.4 %reshape.78 = bf16[5,2,8,4,8,16,8]{6,5,4,3,2,1,0:T(8,128)(2,1)} reshape(bf16[5,16,32,128]{3,2,1,0:T(8,128)(2,1)} %get-tuple-element.8) | data formatting | bytes 1310720 | tf_op jit(solution)/shard_map/reshape | solution.py:96
  93.1 10.7 %copy.18 = bf16[2,4,16,5,8,8,8]{6,5,4,3,2,1,0:T(8,128)(2,1)} copy(bf16[2,4,16,5,8,8,8]{6,2,5,1,4,0,3:T(8,128)(2,1)} %bitcast.69) | data formatting | bytes 1310720 | tf_op jit(solution)/shard_map/transpose | solution.py:99
  103.8 14.5 %reshape.79 = bf16[64,2,2560]{2,1,0:T(2,128)(2,1)} reshape(bf16[2,4,16,5,8,8,8]{6,5,4,3,2,1,0:T(8,128)(2,1)} %copy.18) | data formatting | bytes 1310720 | tf_op jit(solution)/shard_map/reshape | solution.py:99
  118.3 14.4 %reshape.76 = bf16[5,2,8,4,8,16,8]{6,5,4,3,2,1,0:T(8,128)(2,1)} reshape(bf16[5,16,32,128]{3,2,1,0:T(8,128)(2,1)} %get-tuple-element.10) | data formatting | bytes 1310720 | tf_op jit(solution)/shard_map/reshape | solution.py:96
  132.7 10.6 %copy.17 = bf16[2,4,16,5,8,8,8]{6,5,4,3,2,1,0:T(8,128)(2,1)} copy(bf16[2,4,16,5,8,8,8]{6,2,5,1,4,0,3:T(8,128)(2,1)} %bitcast.70) | data formatting | bytes 1310720 | tf_op jit(solution)/shard_map/transpose | solution.py:99
  143.3 14.5 %reshape.77 = bf16[64,2,2560]{2,1,0:T(2,128)(2,1)} reshape(bf16[2,4,16,5,8,8,8]{6,5,4,3,2,1,0:T(8,128)(2,1)} %copy.17) | data formatting | bytes 1310720 | tf_op jit(solution)/shard_map/reshape | solution.py:99
  164.7 4.3 collective-permute-done.11
  169.0 3.5 select_maximum_fusion
  174.8 4.1 fusion.55
  178.9 14.4 %reshape.82 = bf16[5,2,8,4,8,16,8]{6,5,4,3,2,1,0:T(8,128)(2,1)} reshape(bf16[5,16,32,128]{3,2,1,0:T(8,128)(2,1)} %get-tuple-element.6) | data formatting | bytes 1310720 | tf_op jit(solution)/shard_map/reshape | solution.py:96
  193.3 13.3 %copy.19 = bf16[2,4,16,5,8,8,8]{2,1,0,6,5,4,3:T(4,128)(2,1)} copy(bf16[2,4,16,5,8,8,8]{6,2,5,1,4,0,3:T(8,128)(2,1)} %bitcast.71) | data formatting | bytes 1310720 | tf_op jit(solution)/shard_map/transpose | solution.py:99
  206.6 7.3 %reshape.83 = bf16[128,2560]{0,1:T(8,128)(2,1)S(1)} reshape(bf16[2,4,16,5,8,8,8]{2,1,0,6,5,4,3:T(4,128)(2,1)} %copy.19) | data formatting | bytes 1310720 | tf_op jit(solution)/shard_map/reshape | solution.py:99
  215.4 7.8 %scatter_fusion.1 = bf16[128,2,512]{2,1,0:T(2,128)(2,1)} fusion(bf16[128,2,512]{2,1,0:T(2,128)(2,1)} %broadcast_in_dim.41, s32[64]{0:T(128)S(1)} %fusion.52, bf16[64,2,512]{2,1,0:T(2,128)(2,1)S(1)} %reshape.99), kind=kCustom, calls=%fused_computation.1 | custom fusion | bytes 393472 | tf_op jit(solution)/shard_map/scatter | solution.py:139
  223.3 6.9 %all-to-all-start.1 = ((bf16[32,4,2,512]{3,2,1,0:T(2,128)(2,1)}), bf16[32,4,2,512]{3,2,1,0:T(2,128)(2,1)S(1)}, u32[]{:S(2)}, u32[]{:S(2)}) async-start(bf16[32,4,2,512]{3,2,1,0:T(2,128)(2,1)} %bitcast.11), calls=%async_computation.1 | async-start | bytes 524288 | tf_op jit(solution)/shard_map/all_to_all | solution.py:147
  234.0 8.2 %scatter_fusion = bf16[128,2,2560]{2,1,0:T(2,128)(2,1)} fusion(bf16[128,2,2560]{2,1,0:T(2,128)(2,1)} %broadcast_in_dim.39, s32[64]{0:T(128)} %copy-done.13, bf16[64,2,2560]{2,1,0:T(2,128)(2,1)S(1)} %broadcast_select_fusion), kind=kCustom, calls=%fused_computation | custom fusion | bytes 1966336 | tf_op jit(solution)/shard_map/scatter | solution.py:139
  242.2 6.1 %all-to-all-start = ((bf16[32,4,2,2560]{3,2,1,0:T(2,128)(2,1)}), bf16[32,4,2,2560]{3,2,1,0:T(2,128)(2,1)}, u32[]{:S(2)}, u32[]{:S(2)}) async-start(bf16[32,4,2,2560]{3,2,1,0:T(2,128)(2,1)} %bitcast.72), calls=%async_computation | async-start | bytes 2621440 | tf_op jit(solution)/shard_map/all_to_all | solution.py:146
  249.6 29.0 %all-to-all-done = bf16[32,4,2,2560]{3,2,1,0:T(2,128)(2,1)} async-done(((bf16[32,4,2,2560]{3,2,1,0:T(2,128)(2,1)}), bf16[32,4,2,2560]{3,2,1,0:T(2,128)(2,1)}, u32[]{:S(2)}, u32[]{:S(2)}) %all-to-all-start) | async-done | bytes 1310752 | tf_op jit(solution)/shard_map/all_to_all | solution.py:146
  278.7 4.1 reshape.81
  290.9 6.2 %fusion.46 = f32[2560,512]{1,0:T(8,128)} fusion(bf16[256,2560]{1,0:T(8,128)(2,1)} %reshape.81, bf16[256,2048]{1,0:T(8,128)(2,1)} %get-tuple-element.48, bf16[1,512,2048]{2,1,0:T(8,128)(2,1)} %param.12), kind=kOutput, calls=%fused_computation.96 | convolution fusion | flops 1208090624 | bytes 9699328 | tf_op jit(solution)/shard_map/dot_general | solution.py:67
  297.2 92.5 %all-reduce.6.cloned.1.call-done = f32[2560,512]{1,0:T(8,128)} async-done(((f32[2560,512]{1,0:T(8,128)}), f32[2560,512]{1,0:T(8,128)}) %all-reduce.6.cloned.1.call-update) | async-done | bytes 5242896 | tf_op jit(solution)/shard_map/psum | solution.py:159
  389.8 4.1 convolution_bitcast_fusion.1
  396.8 184.4 %all-reduce.8.cloned.1.call-done = f32[2560,512]{1,0:T(8,128)} async-done(((f32[2560,512]{1,0:T(8,128)}), f32[2560,512]{1,0:T(8,128)}) %all-reduce.8.cloned.1.call-update) | async-done | bytes 5242896 | tf_op jit(solution)/shard_map/psum | solution.py:159
  581.2 5.4 copy.41
  (115 shorter events, 57.9 us)
Async XLA Ops:
  7.2 206.8 %copy-start = (bf16[2560,512]{1,0:T(8,128)(2,1)S(1)}, bf16[2560,512]{1,0:T(8,128)(2,1)}, u32[]{:S(2)}) copy-start(bf16[2560,512]{1,0:T(8,128)(2,1)} %param.9) | copy-start | bytes 7864324
  8.4 5.4 collective-permute-start
  10.8 5.4 collective-permute-start.1
  16.3 6.0 %collective-permute-start.2 = (f32[5,20,2,128]{3,2,1,0:T(2,128)S(1)}, f32[5,20,2,128]{3,2,1,0:T(2,128)S(1)}, u32[]{:S(2)}, u32[]{:S(2)}) collective-permute-start(f32[5,20,2,128]{3,2,1,0:T(2,128)S(1)} %get-tuple-element.32), channel_id=1, source_target_pairs={{0,1},{1,2},{2,3},{4,5},{5,6},{6,7},{8,9},{9,10},{10,11},{12,13},{... | collective-permute-start | bytes 307208 | tf_op jit(solution)/shard_map/ppermute | solution.py:27
  20.1 6.6 %collective-permute-start.3 = (f32[5,20,2,128]{3,2,1,0:T(2,128)S(1)}, f32[5,20,2,128]{3,2,1,0:T(2,128)S(1)}, u32[]{:S(2)}, u32[]{:S(2)}) collective-permute-start(f32[5,20,2,128]{3,2,1,0:T(2,128)S(1)} %get-tuple-element.33), channel_id=1, source_target_pairs={{1,0},{2,1},{3,2},{5,4},{6,5},{7,6},{9,8},{10,9},{11,10},{13,12},{... | collective-permute-start | bytes 307208 | tf_op jit(solution)/shard_map/ppermute | solution.py:29
  30.6 1.3 copy-start.6
  31.9 10.4 %copy-start.12 = (s32[64,1]{0,1:T(1,128)S(1)}, s32[64,1]{0,1:T(1,128)}, u32[]{:S(2)}) copy-start(s32[64,1]{0,1:T(1,128)} %param.10) | copy-start | bytes 772
  35.9 1.1 copy-start.3
  37.0 15.6 %collective-permute-start.4 = (f32[5,2,32,128]{3,2,1,0:T(8,128)S(1)}, f32[5,2,32,128]{3,2,1,0:T(8,128)S(1)}, u32[]{:S(2)}, u32[]{:S(2)}) collective-permute-start(f32[5,2,32,128]{3,2,1,0:T(8,128)S(1)} %get-tuple-element.36), channel_id=1, source_target_pairs={{0,4},{4,8},{8,12},{12,16},{16,20},{20,24},{24,28},{1,5},{5,9},{9,... | collective-permute-start | bytes 491528 | tf_op jit(solution)/shard_map/ppermute | solution.py:27
  41.0 11.5 %collective-permute-start.5 = (f32[5,2,32,128]{3,2,1,0:T(8,128)S(1)}, f32[5,2,32,128]{3,2,1,0:T(8,128)S(1)}, u32[]{:S(2)}, u32[]{:S(2)}) collective-permute-start(f32[5,2,32,128]{3,2,1,0:T(8,128)S(1)} %get-tuple-element.37), channel_id=1, source_target_pairs={{4,0},{8,4},{12,8},{16,12},{20,16},{24,20},{28,24},{5,1},{9,5},{13... | collective-permute-start | bytes 491528 | tf_op jit(solution)/shard_map/ppermute | solution.py:29
  42.4 173.1 %copy-start.13 = (s32[64]{0:T(128)}, s32[64]{0:T(128)S(1)}, u32[]{:S(2)}) copy-start(s32[64]{0:T(128)S(1)} %fusion.52) | copy-start | bytes 772
  44.1 179.2 %all-to-all-start.2 = ((bf16[32,1,4]{2,1,0:T(2,128)(2,1)}), bf16[32,1,4]{2,1,0:T(2,128)(2,1)S(1)}, u32[]{:S(2)}, u32[]{:S(2)}) async-start(bf16[32,1,4]{2,1,0:T(2,128)(2,1)} %all_to_all.16), calls=%async_computation.2 | async-start | bytes 32768 | tf_op jit(solution)/shard_map/all_to_all | solution.py:148
  52.6 6.6 %copy-start.4 = (f32[5,16,32,128]{3,2,1,0:T(8,128)S(1)}, f32[5,16,32,128]{3,2,1,0:T(8,128)}, u32[]{:S(2)}) copy-start(f32[5,16,32,128]{3,2,1,0:T(8,128)} %copy-done.3) | copy-start | bytes 3932164
  53.9 6.1 %collective-permute-start.6 = (f32[5,20,2,128]{3,2,1,0:T(2,128)S(1)}, f32[5,20,2,128]{3,2,1,0:T(2,128)S(1)}, u32[]{:S(2)}, u32[]{:S(2)}) collective-permute-start(f32[5,20,2,128]{3,2,1,0:T(2,128)S(1)} %get-tuple-element.30), channel_id=1, source_target_pairs={{0,1},{1,2},{2,3},{4,5},{5,6},{6,7},{8,9},{9,10},{10,11},{12,13},{... | collective-permute-start | bytes 307208 | tf_op jit(solution)/shard_map/ppermute | solution.py:27
  57.5 6.6 %collective-permute-start.7 = (f32[5,20,2,128]{3,2,1,0:T(2,128)S(1)}, f32[5,20,2,128]{3,2,1,0:T(2,128)S(1)}, u32[]{:S(2)}, u32[]{:S(2)}) collective-permute-start(f32[5,20,2,128]{3,2,1,0:T(2,128)S(1)} %get-tuple-element.31), channel_id=1, source_target_pairs={{1,0},{2,1},{3,2},{5,4},{6,5},{7,6},{9,8},{10,9},{11,10},{13,12},{... | collective-permute-start | bytes 307208 | tf_op jit(solution)/shard_map/ppermute | solution.py:29
  69.8 8.1 %copy-start.11 = (s32[2,4,16]{2,1,0:T(4,128)S(1)}, s32[2,4,16]{2,1,0:T(4,128)}, u32[]{:S(2)}) copy-start(s32[2,4,16]{2,1,0:T(4,128)} %param.11) | copy-start | bytes 1540
  73.7 1.1 copy-start.1
  74.8 83.0 %collective-permute-start.8 = (f32[5,2,32,128]{3,2,1,0:T(8,128)S(1)}, f32[5,2,32,128]{3,2,1,0:T(8,128)S(1)}, u32[]{:S(2)}, u32[]{:S(2)}) collective-permute-start(f32[5,2,32,128]{3,2,1,0:T(8,128)S(1)} %get-tuple-element.34), channel_id=1, source_target_pairs={{0,4},{4,8},{8,12},{12,16},{16,20},{20,24},{24,28},{1,5},{5,9},{9,... | collective-permute-start | bytes 491528 | tf_op jit(solution)/shard_map/ppermute | solution.py:27
  76.1 81.7 %collective-permute-start.9 = (f32[5,2,32,128]{3,2,1,0:T(8,128)S(1)}, f32[5,2,32,128]{3,2,1,0:T(8,128)S(1)}, u32[]{:S(2)}, u32[]{:S(2)}) collective-permute-start(f32[5,2,32,128]{3,2,1,0:T(8,128)S(1)} %get-tuple-element.35), channel_id=1, source_target_pairs={{4,0},{8,4},{12,8},{16,12},{20,16},{24,20},{28,24},{5,1},{9,5},{13... | collective-permute-start | bytes 491528 | tf_op jit(solution)/shard_map/ppermute | solution.py:29
  157.8 6.1 %copy-start.2 = (f32[5,16,32,128]{3,2,1,0:T(8,128)S(1)}, f32[5,16,32,128]{3,2,1,0:T(8,128)}, u32[]{:S(2)}) copy-start(f32[5,16,32,128]{3,2,1,0:T(8,128)} %copy-done.1) | copy-start | bytes 3932164
  159.1 5.6 collective-permute-start.10
  162.5 6.6 %collective-permute-start.11 = (f32[5,20,2,128]{3,2,1,0:T(2,128)S(1)}, f32[5,20,2,128]{3,2,1,0:T(2,128)S(1)}, u32[]{:S(2)}, u32[]{:S(2)}) collective-permute-start(f32[5,20,2,128]{3,2,1,0:T(2,128)S(1)} %get-tuple-element.27), channel_id=1, source_target_pairs={{1,0},{2,1},{3,2},{5,4},{6,5},{7,6},{9,8},{10,9},{11,10},{13,12},{... | collective-permute-start | bytes 307208 | tf_op jit(solution)/shard_map/ppermute | solution.py:29
  223.3 19.0 %all-to-all-start.1 = ((bf16[32,4,2,512]{3,2,1,0:T(2,128)(2,1)}), bf16[32,4,2,512]{3,2,1,0:T(2,128)(2,1)S(1)}, u32[]{:S(2)}, u32[]{:S(2)}) async-start(bf16[32,4,2,512]{3,2,1,0:T(2,128)(2,1)} %bitcast.11), calls=%async_computation.1 | async-start | bytes 524288 | tf_op jit(solution)/shard_map/all_to_all | solution.py:147
  242.2 36.4 %all-to-all-start = ((bf16[32,4,2,2560]{3,2,1,0:T(2,128)(2,1)}), bf16[32,4,2,2560]{3,2,1,0:T(2,128)(2,1)}, u32[]{:S(2)}, u32[]{:S(2)}) async-start(bf16[32,4,2,2560]{3,2,1,0:T(2,128)(2,1)} %bitcast.72), calls=%async_computation | async-start | bytes 2621440 | tf_op jit(solution)/shard_map/all_to_all | solution.py:146
  248.3 141.5 %all-reduce.6.cloned.1.call-start = ((), (), s32[]{:S(2)}) async-start(), calls=%async_computation.3 | async-start | bytes 10485760 | tf_op jit(solution)/shard_map/psum | solution.py:159
  282.7 2.3 copy-start.5
  282.7 2.3 copy-start.10
  285.1 1.8 copy-start.14
  285.1 1.8 copy-start.15
  285.8 2.4 copy-start.7
  297.2 284.0 %all-reduce.8.cloned.1.call-start = ((), (), s32[]{:S(2)}) async-start(), calls=%async_computation.4 | async-start | bytes 10485760 | tf_op jit(solution)/shard_map/psum | solution.py:159
  389.8 4.1 copy-start.8
  (1 other events, 1.0 us)
Sparse Core Ops, SparseCore 0:
  297.3 92.3 all-reduce.5
  392.1 188.9 all-reduce.7
